TPU v7x, 64 devices: a 2x2x8 block of a 4x4x8 slice. The times are simulated.
64 devices in a mesh: dp: 8 (over x, y, core), tp: 8 (over z).
Axes of the slice: x: 2, y: 2, z: 8, core: 2. Of those that a mesh axis runs over, the one named last changes fastest.
The devices are a block of a 4x4x8 slice.
Arguments:
- x: bfloat16 [16384, 3072], P('dp'), parts along dimension 0
- w_gate: bfloat16 [3072, 24576], P(None, 'tp')
- w_up: bfloat16 [3072, 24576], P(None, 'tp')
- w_down: bfloat16 [24576, 3072], P('tp')
Outputs:
- output: bfloat16 [16384, 3072], P('dp'), parts along dimension 0
There are 8 independent parts. A program takes and returns all parts, laid end to end along the dimension named above; an argument that names none is the same for every part.
All inputs are finite; a program needn't handle non-finite values.
Results may differ from a plain program's by a relative error of at most 0.016.
Values are sent between devices in bfloat16 or wider.
A program may use at most 768 MiB of HBM per device.

v0:
```python
import jax
import jax.numpy as jnp
from jax import lax
from jax.sharding import PartitionSpec as P


def solution(mesh):
    def step(x, w_gate, w_up, w_down):
        gate = jnp.dot(x, w_gate, preferred_element_type=jnp.float32)
        up = jnp.dot(x, w_up, preferred_element_type=jnp.float32)
        hidden = (jax.nn.gelu(gate) * up).astype(jnp.bfloat16)
        term = jnp.dot(hidden, w_down, preferred_element_type=jnp.float32).astype(jnp.bfloat16)
        return lax.psum(term, "tp")

    return jax.shard_map(
        step,
        mesh=mesh,
        in_specs=(P("dp", None), P(None, "tp"), P(None, "tp"), P("tp", None)),
        out_specs=P("dp", None),
        check_vma=False,
    )
```

profile of v0, /device:TPU:21, one launch (start us, length us, event | category | flops | bytes accessed | tf_op | source)
XLA Modules:
  0.0 438.0 jit_solution(245656149292687142)
XLA Ops:
  6.5 0.0 all-reduce.2.cloned.1.call-start
  6.6 47.7 %fusion.9 = f32[2048,3072]{1,0:T(8,128)} fusion(bf16[2048,3072]{1,0:T(8,128)(2,1)} %param.4, bf16[3072,3072]{1,0:T(8,128)(2,1)} %param.5), kind=kOutput, calls=%fused_computation.11 | convolution fusion | flops 38654705664 | bytes 56623104 | tf_op jit(solution)/shard_map/dot_general | solution.py:9
  54.3 54.8 %fusion.8 = bf16[2048,3072]{1,0:T(8,128)(2,1)} fusion(f32[2048,3072]{1,0:T(8,128)} %fusion.9, bf16[2048,3072]{1,0:T(8,128)(2,1)} %param.4, bf16[3072,3072]{1,0:T(8,128)(2,1)} %param.6), kind=kOutput, calls=%fused_computation.9 | convolution fusion | flops 38717620224 | bytes 69206016 | tf_op jit(solution)/shard_map/dot_general | solution.py:10
  109.0 46.7 %convolution_convert_fusion = bf16[2048,3072]{1,0:T(8,128)(2,1)} fusion(bf16[2048,3072]{1,0:T(8,128)(2,1)} %fusion.8, bf16[3072,3072]{1,0:T(8,128)(2,1)} %param.7), kind=kOutput, calls=%fused_computation.10 | convolution fusion | flops 38660997120 | bytes 44040192 | tf_op jit(solution)/shard_map/dot_general | solution.py:12
  155.8 0.1 all-reduce.2.cloned.1.call-update
  155.9 264.8 %all-reduce.2.cloned.1.call-done = bf16[2048,3072]{1,0:T(8,128)(2,1)} async-done(((bf16[2048,3072]{1,0:T(8,128)(2,1)}), bf16[2048,3072]{1,0:T(8,128)(2,1)}) %all-reduce.2.cloned.1.call-update) | async-done | bytes 12582928 | tf_op jit(solution)/shard_map/psum | solution.py:13
  420.6 10.5 %copy.6 = bf16[2048,3072]{1,0:T(8,128)(2,1)} copy(bf16[2048,3072]{1,0:T(8,128)(2,1)} %all-reduce.2.cloned.1.call-done) | data formatting | bytes 25165824
Async XLA Ops:
  6.5 414.1 %all-reduce.2.cloned.1.call-start = ((), (), s32[]{:S(2)}) async-start(), calls=%async_computation | async-start | bytes 25165824 | tf_op jit(solution)/shard_map/psum | solution.py:13
Sparse Core Ops, SparseCore 0:
  156.0 264.6 all-reduce.1
where the time goes:
time: 438 us
  waiting for transfers between devices  265 us (61%)
  matrix products  149 us (34%)
  between operations  13.4 us (3%)
  local copies, waits for them, and re-layouts  10.5 us (2%)
    psum x1, waiting for transfers between devices, step(): return lax.psum(term, 'tp')  265 us
    dot_general x1, matrix products, step(): up = jnp.dot(x, w_up, preferred_element_type=jnp.float32)  54.8 us
    dot_general x1, matrix products, step(): gate = jnp.dot(x, w_gate, preferred_element_type=jnp.float32)  47.7 us
    dot_general x1, matrix products, step(): jnp.dot(hidden, w_down, preferred_element_type=jnp.float32)  46.7 us
    unnamed x1, local copies, waits for them, and re-layouts  10.5 us
  transfers between devices with their start and end apart: 1, of which 1 were waited for; matrix products, arithmetic and copies ran while one was open for 0% of the time, Pallas kernels for 0%

commit v1 on v0

v1 whole, which is shorter than its diff:
```python
import functools
import math

import jax
import jax.numpy as jnp
from jax import lax
from jax.experimental import pallas as pl
from jax.experimental.pallas import tpu as pltpu
from jax.sharding import PartitionSpec as P

MESH = pl.DeviceIdType.MESH
TILE = 512
SLOTS = 3


def gelu(v):
    c = math.sqrt(2.0 / math.pi)
    return (0.5 * v) * (1.0 + jnp.tanh(v * (c + (c * 0.044715) * (v * v))))


def kernel(
    n, x_ref, wg_hbm, wu_hbm, wd_hbm, y_ref, wg, wu, wd, xb, hb, x_sem, w_sem, d_sem, send_sem, recv_sem
):
    rows, depth = x_ref.shape
    width = wg_hbm.shape[1]
    out = wd_hbm.shape[1]
    block = rows // n
    half = block // 2
    nt = width // TILE
    ct = out // TILE
    me = lax.axis_index("tp")
    right, left = lax.rem(me + 1, n), lax.rem(me + n - 1, n)

    barrier = pltpu.get_barrier_semaphore()
    for neighbour in (left, right):
        pl.semaphore_signal(barrier, inc=1, device_id={"tp": neighbour}, device_id_type=MESH)

    def rows_a(s):
        return pl.ds(pl.multiple_of(lax.rem(me + 2 * n - s, n) * block, block), half)

    def rows_b(s):
        return pl.ds(pl.multiple_of(lax.rem(me + s, n) * block + half, half), half)

    def cols(t):
        return pl.ds(pl.multiple_of(t * TILE, TILE), TILE)

    def x_copies(s):
        return (
            pltpu.make_async_copy(x_ref.at[rows_a(s)], xb.at[pl.ds(0, half)], x_sem.at[0]),
            pltpu.make_async_copy(x_ref.at[rows_b(s)], xb.at[pl.ds(half, half)], x_sem.at[1]),
        )

    def w_copies(t):
        return (
            pltpu.make_async_copy(wg_hbm.at[:, cols(t)], wg.at[t], w_sem.at[0, t]),
            pltpu.make_async_copy(wu_hbm.at[:, cols(t)], wu.at[t], w_sem.at[1, t]),
        )

    def d_copy(q):
        slot = lax.rem(q, SLOTS)
        return pltpu.make_async_copy(wd_hbm.at[:, cols(lax.rem(q, ct))], wd.at[slot], d_sem.at[slot])

    def hop(s, t):
        p = lax.rem(s, 2)
        pair = []
        for d, (at, to) in enumerate(((rows_a(s), right), (rows_b(s), left))):
            ref = y_ref.at[at, cols(t)]
            pair.append(
                pltpu.make_async_remote_copy(
                    src_ref=ref,
                    dst_ref=ref,
                    send_sem=send_sem.at[d, p, t],
                    recv_sem=recv_sem.at[d, p, t],
                    device_id={"tp": to},
                    device_id_type=MESH,
                )
            )
        return pair

    def arrived(s, t):
        p = lax.rem(s, 2)
        for d, at in enumerate((rows_a(s + 1), rows_b(s + 1))):
            ref = y_ref.at[at, cols(t)]
            pltpu.make_async_remote_copy(
                src_ref=ref,
                dst_ref=ref,
                send_sem=send_sem.at[d, p, t],
                recv_sem=recv_sem.at[d, p, t],
                device_id={"tp": right},
                device_id_type=MESH,
            ).wait_recv()

    def sent(s, t):
        for copy in hop(s, t):
            copy.wait_send()

    def gate_up(t, first):
        if first:
            for copy in w_copies(t):
                copy.wait()

            @pl.when(t + 2 < nt)
            def _():
                for copy in w_copies(t + 2):
                    copy.start()

            @pl.when(t + 2 >= nt)
            def _():
                d_copy(t + 2 - nt).start()

        gate = jnp.dot(xb[...], wg[t], preferred_element_type=jnp.float32)
        up = jnp.dot(xb[...], wu[t], preferred_element_type=jnp.float32)
        hb[:, cols(t)] = (gelu(gate) * up).astype(hb.dtype)

    def down(s, t, first):
        q = s * ct + t
        d_copy(q).wait()
        term = jnp.dot(hb[...], wd[lax.rem(q, SLOTS)], preferred_element_type=jnp.float32)

        @pl.when(q + SLOTS < n * ct)
        def _():
            d_copy(q + SLOTS).start()

        upper, lower = term[:half], term[half:]
        if not first:
            arrived(s - 1, t)
            upper += y_ref[rows_a(s), cols(t)].astype(jnp.float32)
            lower += y_ref[rows_b(s), cols(t)].astype(jnp.float32)
        y_ref[rows_a(s), cols(t)] = upper.astype(y_ref.dtype)
        y_ref[rows_b(s), cols(t)] = lower.astype(y_ref.dtype)
        if not first:

            @pl.when(s >= 2)
            def _():
                sent(s - 2, t)

        for copy in hop(s, t):
            copy.start()

    def step(s, first):
        for copy in x_copies(s):
            copy.wait()
        pl.loop(0, nt)(lambda t: gate_up(t, first))

        @pl.when(s + 1 < n)
        def _():
            for copy in x_copies(s + 1):
                copy.start()

        if first:
            for t in range(2, SLOTS):
                d_copy(t).start()
            pl.semaphore_wait(barrier, 2)
        pl.loop(0, ct)(lambda t: down(s, t, first))

    for copy in x_copies(0):
        copy.start()
    for t in range(2):
        for copy in w_copies(t):
            copy.start()
    step(0, True)
    pl.loop(1, n)(lambda s: step(s, False))

    @pl.loop(n, 2 * n - 2)
    def _(s):
        @pl.loop(0, ct)
        def _(t):
            arrived(s - 1, t)
            sent(s - 2, t)
            for copy in hop(s, t):
                copy.start()

    @pl.loop(0, ct)
    def _(t):
        arrived(2 * n - 3, t)
        sent(2 * n - 4, t)
        sent(2 * n - 3, t)


def copy_out(parts, v_ref, o_ref, sem):
    size = v_ref.shape[0] // parts
    copies = [
        pltpu.make_async_copy(v_ref.at[pl.ds(k * size, size)], o_ref.at[pl.ds(k * size, size)], sem.at[k])
        for k in range(parts)
    ]
    for copy in copies:
        copy.start()
    for copy in copies:
        copy.wait()


def solution(mesh):
    n = mesh.shape["tp"]

    def step(x, w_gate, w_up, w_down):
        rows, depth = x.shape
        width, out = w_down.shape
        block = rows // n
        y = pl.pallas_call(
            functools.partial(kernel, n),
            out_shape=pltpu.VMEM((rows, out), x.dtype),
            in_specs=[pl.BlockSpec(memory_space=pl.ANY)] * 4,
            out_specs=pl.BlockSpec(memory_space=pltpu.VMEM),
            scratch_shapes=[
                pltpu.VMEM((width // TILE, depth, TILE), x.dtype),
                pltpu.VMEM((width // TILE, depth, TILE), x.dtype),
                pltpu.VMEM((SLOTS, width, TILE), x.dtype),
                pltpu.VMEM((block, depth), x.dtype),
                pltpu.VMEM((block, width), x.dtype),
                pltpu.SemaphoreType.DMA((2,)),
                pltpu.SemaphoreType.DMA((2, width // TILE)),
                pltpu.SemaphoreType.DMA((SLOTS,)),
                pltpu.SemaphoreType.DMA((2, 2, out // TILE)),
                pltpu.SemaphoreType.DMA((2, 2, out // TILE)),
            ],
            compiler_params=pltpu.CompilerParams(
                collective_id=0, has_side_effects=True, vmem_limit_bytes=67043328 - rows * out * 2
            ),
        )(x, w_gate, w_up, w_down)
        return pl.pallas_call(
            functools.partial(copy_out, n),
            out_shape=jax.ShapeDtypeStruct(y.shape, y.dtype),
            in_specs=[pl.BlockSpec(memory_space=pltpu.VMEM)],
            out_specs=pl.BlockSpec(memory_space=pl.ANY),
            scratch_shapes=[pltpu.SemaphoreType.DMA((n,))],
            compiler_params=pltpu.CompilerParams(vmem_limit_bytes=1 << 20),
        )(y)

    return jax.shard_map(
        step,
        mesh=mesh,
        in_specs=(P("dp", None), P(None, "tp"), P(None, "tp"), P("tp", None)),
        out_specs=P("dp", None),
        check_vma=False,
    )
```

time: 438 us -> 271 us (0.62)
  Pallas kernels: 0 us -> 271 us
  waiting for transfers between devices: 265 us -> 0 us
  matrix products: 149 us -> 0 us
  between operations: 13.4 us -> 0.01 us
  local copies, waits for them, and re-layouts: 10.5 us -> 0 us
    pallas_call x0 -> x2, Pallas kernels: none -> 271 us  [the longest x1 266 us: step(): pl.pallas_call(functools.partial(kernel, n), out_shape=pltpu.VMEM((rows,...]
    psum x1 -> x0, waiting for transfers between devices: 265 us -> none  [step(): return lax.psum(term, 'tp')]
    dot_general x3 -> x0, matrix products: 149 us -> none  [the longest x1 54.8 us: step(): up = jnp.dot(x, w_up, preferred_element_type=jnp.float32)]
    unnamed x1 -> x0, local copies, waits for them, and re-layouts: 10.5 us -> none
  transfers between devices with their start and end apart: 1 -> 0, of which waited for: 1 -> 0; matrix products, arithmetic and copies ran while one was open for 0% -> 0% of each run, Pallas kernels for 0% -> 0%
where the time goes in v1:
time: 271 us
  Pallas kernels  271 us (100%)
    pallas_call x1, Pallas kernels, step(): pl.pallas_call(functools.partial(kernel, n), out_shape=pltpu.VMEM((rows,...  266 us

profile of v1, /device:TPU:21, one launch (start us, length us, event | category | flops | bytes accessed | tf_op | source)
XLA Modules:
  0.0 270.7 jit_solution(15693121420840684677)
XLA Ops:
  0.0 266.0 %shard_map.46.v_ref = bf16[2048,3072]{1,0:T(8,128)(2,1)S(1)} custom-call(bf16[2048,3072]{1,0:T(8,128)(2,1)} %x_ref.1, bf16[3072,3072]{1,0:T(8,128)(2,1)} %wg_hbm.1, bf16[3072,3072]{1,0:T(8,128)(2,1)} %wu_hbm.1, bf16[3072,3072]{1,0:T(8,128)(2,1)} %wd_hbm.1), custom_call_target="tpu_custom_call" | custom-call | tf_op jit(solution)/shard_map/pallas_call | solution.py:199
  266.0 4.7 %shard_map.47 = bf16[2048,3072]{1,0:T(8,128)(2,1)} custom-call(bf16[2048,3072]{1,0:T(8,128)(2,1)S(1)} %shard_map.46.v_ref), custom_call_target="tpu_custom_call" | custom-call | tf_op jit(solution)/shard_map/pallas_call | solution.py:220

commit v2 on v1

--- a/solution.py
+++ b/solution.py
@@ -10,7 +10,7 @@
 
 MESH = pl.DeviceIdType.MESH
 TILE = 512
-SLOTS = 3
+SLOTS = 2
 
 
 def gelu(v):
@@ -45,9 +45,10 @@
         return pl.ds(pl.multiple_of(t * TILE, TILE), TILE)
 
     def x_copies(s):
+        p = lax.rem(s, 2)
         return (
-            pltpu.make_async_copy(x_ref.at[rows_a(s)], xb.at[pl.ds(0, half)], x_sem.at[0]),
-            pltpu.make_async_copy(x_ref.at[rows_b(s)], xb.at[pl.ds(half, half)], x_sem.at[1]),
+            pltpu.make_async_copy(x_ref.at[rows_a(s)], xb.at[p, pl.ds(0, half)], x_sem.at[p, 0]),
+            pltpu.make_async_copy(x_ref.at[rows_b(s)], xb.at[p, pl.ds(half, half)], x_sem.at[p, 1]),
         )
 
     def w_copies(t):
@@ -69,7 +70,7 @@
                 pltpu.make_async_remote_copy(
                     src_ref=ref,
                     dst_ref=ref,
-                    send_sem=send_sem.at[d, p, t],
+                    send_sem=send_sem.at[d, t],
                     recv_sem=recv_sem.at[d, p, t],
                     device_id={"tp": to},
                     device_id_type=MESH,
@@ -84,7 +85,7 @@
             pltpu.make_async_remote_copy(
                 src_ref=ref,
                 dst_ref=ref,
-                send_sem=send_sem.at[d, p, t],
+                send_sem=send_sem.at[d, t],
                 recv_sem=recv_sem.at[d, p, t],
                 device_id={"tp": right},
                 device_id_type=MESH,
@@ -94,86 +95,124 @@
         for copy in hop(s, t):
             copy.wait_send()
 
-    def gate_up(t, first):
-        if first:
-            for copy in w_copies(t):
-                copy.wait()
-
-            @pl.when(t + 2 < nt)
-            def _():
-                for copy in w_copies(t + 2):
-                    copy.start()
-
-            @pl.when(t + 2 >= nt)
-            def _():
-                d_copy(t + 2 - nt).start()
-
-        gate = jnp.dot(xb[...], wg[t], preferred_element_type=jnp.float32)
-        up = jnp.dot(xb[...], wu[t], preferred_element_type=jnp.float32)
-        hb[:, cols(t)] = (gelu(gate) * up).astype(hb.dtype)
-
-    def down(s, t, first):
-        q = s * ct + t
-        d_copy(q).wait()
-        term = jnp.dot(hb[...], wd[lax.rem(q, SLOTS)], preferred_element_type=jnp.float32)
-
-        @pl.when(q + SLOTS < n * ct)
-        def _():
-            d_copy(q + SLOTS).start()
-
-        upper, lower = term[:half], term[half:]
-        if not first:
-            arrived(s - 1, t)
-            upper += y_ref[rows_a(s), cols(t)].astype(jnp.float32)
-            lower += y_ref[rows_b(s), cols(t)].astype(jnp.float32)
-        y_ref[rows_a(s), cols(t)] = upper.astype(y_ref.dtype)
-        y_ref[rows_b(s), cols(t)] = lower.astype(y_ref.dtype)
-        if not first:
-
-            @pl.when(s >= 2)
-            def _():
-                sent(s - 2, t)
-
+    def gate_up(s, t):
+        p = lax.rem(s, 2)
+        gate = jnp.dot(xb[p], wg[t], preferred_element_type=jnp.float32)
+        up = jnp.dot(xb[p], wu[t], preferred_element_type=jnp.float32)
+        hb[p, :, cols(t)] = (gelu(gate) * up).astype(hb.dtype)
+
+    def down(s, t, first=False):
+        slot = lax.rem(s * ct + t, SLOTS)
+        for k, at in enumerate((rows_a(s), rows_b(s))):
+            part = jnp.dot(hb[lax.rem(s, 2), pl.ds(k * half, half)], wd[slot], preferred_element_type=jnp.float32)
+            if not first:
+                part += y_ref[at, cols(t)].astype(jnp.float32)
+            y_ref[at, cols(t)] = part.astype(y_ref.dtype)
+
+    def ready(s, t):
+        d_copy(s * ct + t).wait()
+        arrived(s - 1, t)
+        sent(s - 1, t)
+
+    def send(s, t):
         for copy in hop(s, t):
             copy.start()
 
-    def step(s, first):
-        for copy in x_copies(s):
+    def begin(s):
+        for copy in x_copies(s + 1):
             copy.wait()
-        pl.loop(0, nt)(lambda t: gate_up(t, first))
-
-        @pl.when(s + 1 < n)
-        def _():
-            for copy in x_copies(s + 1):
-                copy.start()
-
-        if first:
-            for t in range(2, SLOTS):
-                d_copy(t).start()
-            pl.semaphore_wait(barrier, 2)
-        pl.loop(0, ct)(lambda t: down(s, t, first))
+
+        @pl.when(s + 2 < n)
+        def _():
+            for copy in x_copies(s + 2):
+                copy.start()
 
     for copy in x_copies(0):
         copy.start()
-    for t in range(2):
+    for copy in w_copies(0):
+        copy.start()
+    for copy in x_copies(0):
+        copy.wait()
+    for copy in w_copies(1):
+        copy.start()
+
+    @pl.loop(0, nt)
+    def _(t):
         for copy in w_copies(t):
-            copy.start()
-    step(0, True)
-    pl.loop(1, n)(lambda s: step(s, False))
+            copy.wait()
+
+        @pl.when(t + 2 < nt)
+        def _():
+            for copy in w_copies(t + 2):
+                copy.start()
+
+        @pl.when(t + 2 == nt)
+        def _():
+            d_copy(0).start()
+
+        @pl.when(t + 1 == nt)
+        def _():
+            for copy in x_copies(1):
+                copy.start()
+            for q in range(1, SLOTS):
+                d_copy(q).start()
+
+        gate_up(0, t)
+
+    pl.semaphore_wait(barrier, 2)
+
+    def down_alone(s, t):
+        ready(s, t)
+        down(s, t)
+        send(s, t)
+        d_copy(s * ct + t + SLOTS).start()
+
+    @pl.loop(0, ct)
+    def _(t):
+        d_copy(t).wait()
+        down(0, t, True)
+        send(0, t)
+        d_copy(t + SLOTS).start()
+
+        @pl.when(t == 0)
+        def _():
+            begin(0)
+
+        gate_up(1, t)
+
+    down_alone(1, 0)
+
+    @pl.loop(1, n - 1)
+    def _(s):
+        begin(s)
+
+        @pl.loop(1, ct)
+        def _(t):
+            ready(s, t)
+            down(s, t)
+            gate_up(s + 1, t - 1)
+            send(s, t)
+            d_copy(s * ct + t + SLOTS).start()
+
+        gate_up(s + 1, nt - 1)
+        down_alone(s + 1, 0)
+
+    pl.loop(1, ct)(lambda t: down_alone(n - 1, t))
+    for t in range(SLOTS):
+        d_copy(n * ct + t).wait()
 
     @pl.loop(n, 2 * n - 2)
     def _(s):
         @pl.loop(0, ct)
         def _(t):
             arrived(s - 1, t)
-            sent(s - 2, t)
+            sent(s - 1, t)
             for copy in hop(s, t):
                 copy.start()
 
     @pl.loop(0, ct)
     def _(t):
         arrived(2 * n - 3, t)
-        sent(2 * n - 4, t)
         sent(2 * n - 3, t)
 
 
@@ -205,12 +244,12 @@
                 pltpu.VMEM((width // TILE, depth, TILE), x.dtype),
                 pltpu.VMEM((width // TILE, depth, TILE), x.dtype),
                 pltpu.VMEM((SLOTS, width, TILE), x.dtype),
-                pltpu.VMEM((block, depth), x.dtype),
-                pltpu.VMEM((block, width), x.dtype),
-                pltpu.SemaphoreType.DMA((2,)),
+                pltpu.VMEM((2, block, depth), x.dtype),
+                pltpu.VMEM((2, block, width), x.dtype),
+                pltpu.SemaphoreType.DMA((2, 2)),
                 pltpu.SemaphoreType.DMA((2, width // TILE)),
                 pltpu.SemaphoreType.DMA((SLOTS,)),
-                pltpu.SemaphoreType.DMA((2, 2, out // TILE)),
+                pltpu.SemaphoreType.DMA((2, out // TILE)),
                 pltpu.SemaphoreType.DMA((2, 2, out // TILE)),
             ],
             compiler_params=pltpu.CompilerParams(

time: 271 us -> 266 us (0.982)
  Pallas kernels: 271 us -> 266 us
    pallas_call x1, Pallas kernels: 266 us -> 262 us  [step(): pl.pallas_call(functools.partial(kernel, n), out_shape=pltpu.VMEM((rows,...]
where the time goes in v2:
time: 266 us
  Pallas kernels  266 us (100%)
    pallas_call x1, Pallas kernels, step(): pl.pallas_call(functools.partial(kernel, n), out_shape=pltpu.VMEM((rows,...  262 us

profile of v2, /device:TPU:21, one launch (start us, length us, event | category | flops | bytes accessed | tf_op | source)
XLA Modules:
  0.0 266.3 jit_solution(10160735208466730175)
XLA Ops:
  0.0 261.6 %shard_map.46.v_ref = bf16[2048,3072]{1,0:T(8,128)(2,1)S(1)} custom-call(bf16[2048,3072]{1,0:T(8,128)(2,1)} %x_ref.1, bf16[3072,3072]{1,0:T(8,128)(2,1)} %wg_hbm.1, bf16[3072,3072]{1,0:T(8,128)(2,1)} %wu_hbm.1, bf16[3072,3072]{1,0:T(8,128)(2,1)} %wd_hbm.1), custom_call_target="tpu_custom_call" | custom-call | tf_op jit(solution)/shard_map/pallas_call | solution.py:238
  261.6 4.7 %shard_map.47 = bf16[2048,3072]{1,0:T(8,128)(2,1)} custom-call(bf16[2048,3072]{1,0:T(8,128)(2,1)S(1)} %shard_map.46.v_ref), custom_call_target="tpu_custom_call" | custom-call | tf_op jit(solution)/shard_map/pallas_call | solution.py:259

commit v3 on v2

--- a/solution.py
+++ b/solution.py
@@ -112,9 +112,10 @@
     def ready(s, t):
         d_copy(s * ct + t).wait()
         arrived(s - 1, t)
-        sent(s - 1, t)
-
-    def send(s, t):
+
+    def send(s, t, first=False):
+        if not first:
+            sent(s - 1, t)
         for copy in hop(s, t):
             copy.start()
 
@@ -171,7 +172,7 @@
     def _(t):
         d_copy(t).wait()
         down(0, t, True)
-        send(0, t)
+        send(0, t, True)
         d_copy(t + SLOTS).start()
 
         @pl.when(t == 0)

time: 266 us -> 267 us (level)
  no operation moved by 1% of the time
where the time goes in v3:
time: 267 us; the launch traced here: 266 us
  Pallas kernels  266 us (100%)
    pallas_call x1, Pallas kernels, step(): pl.pallas_call(functools.partial(kernel, n), out_shape=pltpu.VMEM((rows,...  262 us

profile of v3, /device:TPU:21, one launch (start us, length us, event | category | flops | bytes accessed | tf_op | source)
XLA Modules:
  0.0 266.3 jit_solution(5631135110780999533)
XLA Ops:
  0.0 261.7 %shard_map.46.v_ref = bf16[2048,3072]{1,0:T(8,128)(2,1)S(1)} custom-call(bf16[2048,3072]{1,0:T(8,128)(2,1)} %x_ref.1, bf16[3072,3072]{1,0:T(8,128)(2,1)} %wg_hbm.1, bf16[3072,3072]{1,0:T(8,128)(2,1)} %wu_hbm.1, bf16[3072,3072]{1,0:T(8,128)(2,1)} %wd_hbm.1), custom_call_target="tpu_custom_call" | custom-call | tf_op jit(solution)/shard_map/pallas_call | solution.py:239
  261.7 4.7 %shard_map.47 = bf16[2048,3072]{1,0:T(8,128)(2,1)} custom-call(bf16[2048,3072]{1,0:T(8,128)(2,1)S(1)} %shard_map.46.v_ref), custom_call_target="tpu_custom_call" | custom-call | tf_op jit(solution)/shard_map/pallas_call | solution.py:260
